TPU v7x, 256 devices: a whole 4x4x8 slice. The times are simulated.
256 devices in a mesh: dp: 32 (over y, x, core), seq: 8 (over z).
Axes of the slice: x: 4, y: 4, z: 8, core: 2. Of those that a mesh axis runs over, the one named last changes fastest.
Arguments:
- query_rows: bfloat16 [32, 1024, 3072], P('dp', 'seq'), may hold values from -6 to 6
- key_rows: bfloat16 [32, 1024, 3072], P('dp', 'seq'), may hold values from -6 to 6
- value_rows: bfloat16 [32, 1024, 3072], P('dp', 'seq'), may hold values from -6 to 6
- out_grad: bfloat16 [32, 1024, 6144], P('dp', 'seq'), may hold values from -54 to 54
- clip_lengths: int32 [32, 4], P('dp'), may hold values from 1 to 512, 1024 in all within a row
- out_weight: bfloat16 [3072, 6144], P('seq'), may hold values from -0.109375 to 0.109375
- query_gain: float32 [128], replicated, may hold values from 0.1 to 1.9
- key_gain: float32 [128], replicated, may hold values from 0.1 to 1.9
Outputs:
- query_grad: bfloat16 [32, 1024, 3072], P('dp', 'seq')
- key_grad: bfloat16 [32, 1024, 3072], P('dp', 'seq')
- value_grad: bfloat16 [32, 1024, 3072], P('dp', 'seq')
- weight_grad: float32 [3072, 6144], P('seq', 'dp')
- querygain_grad: float32 [128], replicated
- keygain_grad: float32 [128], replicated
- grad_norm: float32 [], replicated
Inputs may be any that keep to these rules, and one draw needn't show every extreme that they name: `clip_lengths`: the token counts of each group's clips sum to 1024.
All inputs are finite; a program needn't handle non-finite values.
Results may differ from a plain program's by a relative error of at most 0.015.
Values may be sent and summed in bfloat16 or wider, within the bound.
A program may use at most 128 MiB of HBM per device.

v0:
```python
import jax
import jax.numpy as jnp
from jax import lax
from jax.sharding import Mesh
from jax.sharding import PartitionSpec as P

HEAD_DIM = 128
MAX_NORM = 768
DP = ("dp_0", "dp_1", "dp_2")
DP_SEQ = ("dp_0", "dp_1", "dp_2", "seq")
EPS = 1e-06


def one_axis_at_a_time(array, axes):
    for axis in axes:
        array = lax.psum(array, axis)
    return array


def segment_ids(lengths, total):
    ends = jnp.cumsum(lengths)
    places = jnp.arange(total, dtype=jnp.int32)
    return jnp.sum((places[:, None] >= ends[None, :]).astype(jnp.int32), axis=1)


def norm_rows(rows, gain):
    wide = rows.astype(jnp.float32)
    inverse = lax.rsqrt(jnp.mean(wide * wide, axis=-1, keepdims=True) + EPS)
    unit = wide * inverse
    return (unit, inverse, (unit * gain).astype(jnp.bfloat16))


def norm_back(unit, inverse, gain, d_norm):
    gain_part = jnp.sum(unit * d_norm, axis=(0, 1))
    d_unit = d_norm * gain
    d_rows = inverse * (d_unit - unit * jnp.mean(unit * d_unit, axis=-1, keepdims=True))
    return (d_rows.astype(jnp.bfloat16), gain_part)


def local(
    query_rows, key_rows, value_rows, out_grad, clip_lengths, out_weight, query_gain, key_gain
):
    query, keys, values = (
        lax.all_to_all(query_rows[0], "seq", split_axis=1, concat_axis=0, tiled=True),
        lax.all_to_all(key_rows[0], "seq", split_axis=1, concat_axis=0, tiled=True),
        lax.all_to_all(value_rows[0], "seq", split_axis=1, concat_axis=0, tiled=True),
    )
    total = query.shape[0]
    heads = query.shape[1] // HEAD_DIM
    width = heads * HEAD_DIM
    scale = HEAD_DIM ** (-0.5)
    block = min(512, total)
    blocks = total // block
    seg = segment_ids(clip_lengths[0], total)
    q_unit, q_inv, q_norm = norm_rows(query.reshape(total, heads, HEAD_DIM), query_gain)
    k_unit, k_inv, k_norm = norm_rows(keys.reshape(total, heads, HEAD_DIM), key_gain)
    values3 = values.reshape(total, heads, HEAD_DIM)

    def forward_block(index):
        start = index * block
        query_block = lax.dynamic_slice_in_dim(q_norm, start, block, 0)
        seg_block = lax.dynamic_slice_in_dim(seg, start, block, 0)
        scores = (
            jnp.einsum("qhd,khd->hqk", query_block, k_norm, preferred_element_type=jnp.float32)
            * scale
        )
        same = seg_block[:, None] == seg[None, :]
        expo = jnp.where(same[None], jnp.exp(scores), 0.0)
        probs = (expo / jnp.sum(expo, axis=-1, keepdims=True)).astype(jnp.bfloat16)
        attn_out = jnp.einsum("hqk,khd->qhd", probs, values3, preferred_element_type=jnp.float32)
        return (probs, attn_out.astype(jnp.bfloat16))

    probs_all, attn_blocks = lax.map(forward_block, jnp.arange(blocks, dtype=jnp.int32))
    attn_flat = attn_blocks.reshape(total, width)
    out_full = lax.all_gather(out_grad[0], "seq", axis=0, tiled=True)
    weight_part = jnp.dot(attn_flat.T, out_full, preferred_element_type=jnp.float32)
    d_attn = jnp.dot(out_full, out_weight.T, preferred_element_type=jnp.float32).astype(
        jnp.bfloat16
    )
    d_attn3 = d_attn.reshape(total, heads, HEAD_DIM)

    def backward_block(carry, items):
        d_key, d_value = carry
        probs, index = items
        start = index * block
        attn_grad = lax.dynamic_slice_in_dim(d_attn3, start, block, 0)
        query_block = lax.dynamic_slice_in_dim(q_norm, start, block, 0)
        d_probs = jnp.einsum("qhd,khd->hqk", attn_grad, values3, preferred_element_type=jnp.float32)
        probs32 = probs.astype(jnp.float32)
        row_sum = jnp.sum(probs32 * d_probs, axis=-1, keepdims=True)
        d_scores = (probs32 * (d_probs - row_sum) * scale).astype(jnp.bfloat16)
        d_value = d_value + jnp.einsum(
            "hqk,qhd->khd", probs, attn_grad, preferred_element_type=jnp.float32
        )
        d_key = d_key + jnp.einsum(
            "hqk,qhd->khd", d_scores, query_block, preferred_element_type=jnp.float32
        )
        d_query = jnp.einsum("hqk,khd->qhd", d_scores, k_norm, preferred_element_type=jnp.float32)
        return ((d_key, d_value), d_query)

    empty = jnp.zeros((total, heads, HEAD_DIM), jnp.float32)
    (d_knorm, d_value32), d_query_blocks = lax.scan(
        backward_block, (empty, empty), (probs_all, jnp.arange(blocks, dtype=jnp.int32))
    )
    d_qnorm = d_query_blocks.reshape(total, heads, HEAD_DIM)
    query_grad, q_gain_part = norm_back(q_unit, q_inv, query_gain, d_qnorm)
    key_grad, k_gain_part = norm_back(k_unit, k_inv, key_gain, d_knorm)
    value_grad = d_value32.astype(jnp.bfloat16)
    query_back, key_back, value_back = (
        lax.all_to_all(
            query_grad.reshape(total, width), "seq", split_axis=0, concat_axis=1, tiled=True
        ),
        lax.all_to_all(
            key_grad.reshape(total, width), "seq", split_axis=0, concat_axis=1, tiled=True
        ),
        lax.all_to_all(
            value_grad.reshape(total, width), "seq", split_axis=0, concat_axis=1, tiled=True
        ),
    )
    weight_shard = lax.psum_scatter(
        weight_part.astype(jnp.bfloat16), DP, scatter_dimension=1, tiled=True
    ).astype(jnp.float32)
    local_squares = jnp.sum(weight_shard * weight_shard)
    qgain_raw, kgain_raw = (
        one_axis_at_a_time(q_gain_part, DP_SEQ),
        one_axis_at_a_time(k_gain_part, DP_SEQ),
    )
    weight_squares = one_axis_at_a_time(local_squares, DP_SEQ)
    squares = weight_squares + jnp.sum(qgain_raw * qgain_raw) + jnp.sum(kgain_raw * kgain_raw)
    grad_norm = jnp.sqrt(squares)
    factor = jnp.minimum(jnp.float32(1.0), MAX_NORM / (grad_norm + EPS))
    return (
        query_back[None],
        key_back[None],
        value_back[None],
        weight_shard * factor,
        qgain_raw * factor,
        kgain_raw * factor,
        grad_norm,
    )


def solution(mesh):
    torus = Mesh(mesh.devices.reshape(4, 4, 2, mesh.shape["seq"]), ("dp_0", "dp_1", "dp_2", "seq"))
    return jax.shard_map(
        local,
        mesh=torus,
        in_specs=(
            P(DP, "seq", None),
            P(DP, "seq", None),
            P(DP, "seq", None),
            P(DP, "seq", None),
            P(DP, None),
            P("seq", None),
            P(),
            P(),
        ),
        out_specs=(
            P(DP, "seq", None),
            P(DP, "seq", None),
            P(DP, "seq", None),
            P("seq", DP),
            P(),
            P(),
            P(),
        ),
        check_vma=False,
    )
```

profile of v0, /device:TPU:32, one launch (start us, length us, event | category | flops | bytes accessed | tf_op | source)
XLA Modules:
  0.0 430.5 jit_solution(6281215837916845542)
XLA Ops:
  9.5 8.6 %all-to-all-start = ((bf16[128,8,384]{0,2,1:T(8,128)(2,1)}), bf16[128,8,384]{0,2,1:T(8,128)(2,1)S(1)}, u32[]{:S(2)}, u32[]{:S(2)}) async-start(bf16[128,8,384]{0,2,1:T(8,128)(2,1)} %bitcast.4), calls=%async_computation | async-start | bytes 1572864 | tf_op jit(solution)/shard_map/all_to_all | solution.py:44
  19.2 26.2 %all-to-all-done = bf16[128,8,384]{0,2,1:T(8,128)(2,1)S(1)} async-done(((bf16[128,8,384]{0,2,1:T(8,128)(2,1)}), bf16[128,8,384]{0,2,1:T(8,128)(2,1)S(1)}, u32[]{:S(2)}, u32[]{:S(2)}) %all-to-all-start) | async-done | bytes 786464 | tf_op jit(solution)/shard_map/all_to_all | solution.py:44
  45.4 5.8 %all-to-all-start.1 = ((bf16[128,8,384]{0,2,1:T(8,128)(2,1)}), bf16[128,8,384]{0,2,1:T(8,128)(2,1)S(1)}, u32[]{:S(2)}, u32[]{:S(2)}) async-start(bf16[128,8,384]{0,2,1:T(8,128)(2,1)} %bitcast.8), calls=%async_computation.1 | async-start | bytes 1572864 | tf_op jit(solution)/shard_map/all_to_all | solution.py:45
  52.3 30.0 %all-to-all-done.1 = bf16[128,8,384]{0,2,1:T(8,128)(2,1)S(1)} async-done(((bf16[128,8,384]{0,2,1:T(8,128)(2,1)}), bf16[128,8,384]{0,2,1:T(8,128)(2,1)S(1)}, u32[]{:S(2)}, u32[]{:S(2)}) %all-to-all-start.1) | async-done | bytes 786464 | tf_op jit(solution)/shard_map/all_to_all | solution.py:45
  82.4 5.3 %all-to-all-start.2 = ((bf16[128,8,384]{0,2,1:T(8,128)(2,1)}), bf16[128,8,384]{0,2,1:T(8,128)(2,1)}, u32[]{:S(2)}, u32[]{:S(2)}) async-start(bf16[128,8,384]{0,2,1:T(8,128)(2,1)} %bitcast.10), calls=%async_computation.2 | async-start | bytes 1572864 | tf_op jit(solution)/shard_map/all_to_all | solution.py:46
  92.0 2.1 copy.147
  97.4 2.3 copy.151
  99.7 19.1 %all-to-all-done.2 = bf16[128,8,384]{0,2,1:T(8,128)(2,1)} async-done(((bf16[128,8,384]{0,2,1:T(8,128)(2,1)}), bf16[128,8,384]{0,2,1:T(8,128)(2,1)}, u32[]{:S(2)}, u32[]{:S(2)}) %all-to-all-start.2) | async-done | bytes 786464 | tf_op jit(solution)/shard_map/all_to_all | solution.py:46
  118.7 2.5 copy.149
  121.2 2.2 reshape.177
  123.4 2.3 copy.152
  128.8 21.1 %while.27 = (s32[]{:T(128)}, bf16[2,3,512,1024]{3,2,1,0:T(8,128)(2,1)}, bf16[2,512,3,128]{3,1,2,0:T(8,128)(2,1)}, s32[2]{0:T(128)S(1)}, s32[1024]{0:T(1024)S(1)}...) while((s32[]{:T(128)}, ...), condition=%wide.region_6.7_spmd, body=%wide.region_4.6_spmd.sunk | while | flops 817035776 | bytes 85746000 | solution.py:73
  130.5 3.4 fusion.75
  141.1 3.4 fusion.75
  149.9 3.1 copy.167
  153.0 2.1 copy.180
  156.8 32.1 %all-gather.3.cloned.1.call-done = bf16[1,1024,6144]{2,1,0:T(8,128)(2,1)} async-done(((bf16[1,128,6144]{2,1,0:T(8,128)(2,1)}), bf16[1,1024,6144]{2,1,0:T(8,128)(2,1)}) %all-gather.3.cloned.1.call-update) | async-done | bytes 12582928 | tf_op jit(solution)/shard_map/all_gather | solution.py:75
  188.9 11.4 %fusion.42 = bf16[384,6144]{0,1:T(8,128)(2,1)} fusion(bf16[1024,384]{0,1:T(8,128)(2,1)} %bitcast.161, bf16[1,1024,6144]{2,1,0:T(8,128)(2,1)} %all-gather.3.cloned.1.call-done), kind=kOutput, calls=%fused_computation.45 | convolution fusion | flops 4834197504 | bytes 18087936 | tf_op jit(solution)/shard_map/dot_general | solution.py:76
  200.3 10.4 %fusion.48 = bf16[1024,384]{0,1:T(8,128)(2,1)} fusion(bf16[384,6144]{1,0:T(8,128)(2,1)} %param.17, bf16[1,1024,6144]{2,1,0:T(8,128)(2,1)} %all-gather.3.cloned.1.call-done), kind=kOutput, calls=%fused_computation.62 | convolution fusion | flops 4832231424 | bytes 18087936 | tf_op jit(solution)/shard_map/dot_general | solution.py:77
  210.8 57.7 %while.28 = (s32[]{:T(128)}, f32[1024,3,128]{0,2,1:T(8,128)}, f32[1024,3,128]{0,2,1:T(8,128)S(1)}, f32[2,512,3,128]{3,1,2,0:T(8,128)}, s32[2]{0:T(128)S(1)}, /*i...) while((s32[]{:T(128)}, f32[1024,3,128]{0,2,1:T(8,128)}, ...), condition=%wide.region_9.10_spmd.clone, body=%wide.region_7.9_spmd.clone.sunk | while | flops 1634210816 | bytes 57019604 | solution.py:102
  212.0 5.0 %fusion.83 = f32[3,512,1024]{2,1,0:T(8,128)} fusion(bf16[1024,3,128]{2,0,1:T(8,128)(2,1)} %get-tuple-element.549, bf16[1024,3,128]{0,2,1:T(8,128)(2,1)} %get-tuple-element.548, s32[]{:T(128)S(6)} %select_n.24), kind=kOutput, calls=%fused_computation.30.clone.1 | convolution fusion | flops 402653184 | bytes 7471108 | tf_op jit(solution)/shard_map/while/body/eval_jaxpr/qhd,khd->hqk/dot_general | solution.py:88
  217.0 10.2 %bitcast_add_fusion.4 = f32[1024,3,128]{0,2,1:T(8,128)} fusion(f32[1024,3,128]{0,2,1:T(8,128)} %get-tuple-element.528, f32[3,512,1024]{2,1,0:T(8,128)} %fusion.83, bf16[2,3,512,1024]{3,2,1,0:T(8,128)(2,1)} %get-tuple-element.547, s32[]{:T(128)} %get-tuple-element.527, pred[]{:T(512)S(6)} %compare.3, bf16[1024,3,128]{0,2,1:T(8,128)(2,1)} %get-tuple-element.546, ...), kind=kOutput, calls=%fused_computation.26.clone.1 | convolution fusion | flops 414452224 | bytes 22414340 | tf_op jit(solution)/shard_map/while/body/eval_jaxpr/hqk,qhd->khd/dot_general | solution.py:95
  227.2 9.7 %fusion.84 = f32[2,512,3,128]{3,1,2,0:T(8,128)} fusion(f32[2,512,3,128]{3,1,2,0:T(8,128)} %get-tuple-element.530, s32[]{:T(128)} %get-tuple-element.527, bf16[1024,3,128]{2,0,1:T(8,128)(2,1)} %get-tuple-element.550, f32[3,512,1024]{2,1,0:T(8,128)} %fusion.83, bf16[2,3,512,1024]{3,2,1,0:T(8,128)(2,1)} %get-tuple-element.547), kind=kOutput, calls=%fused_computation.28.clone.1 | convolution fusion | flops 413665792 | bytes 20448768 | tf_op jit(solution)/shard_map/while/body/eval_jaxpr/hqk,khd->qhd/dot_general | solution.py:98
  236.9 3.0 bitcast_add_fusion.5
  241.2 4.9 %fusion.83 = f32[3,512,1024]{2,1,0:T(8,128)} fusion(bf16[1024,3,128]{2,0,1:T(8,128)(2,1)} %get-tuple-element.549, bf16[1024,3,128]{0,2,1:T(8,128)(2,1)} %get-tuple-element.548, s32[]{:T(128)S(6)} %select_n.24), kind=kOutput, calls=%fused_computation.30.clone.1 | convolution fusion | flops 402653184 | bytes 7471108 | tf_op jit(solution)/shard_map/while/body/eval_jaxpr/qhd,khd->hqk/dot_general | solution.py:88
  246.1 10.1 %bitcast_add_fusion.4 = f32[1024,3,128]{0,2,1:T(8,128)} fusion(f32[1024,3,128]{0,2,1:T(8,128)} %get-tuple-element.528, f32[3,512,1024]{2,1,0:T(8,128)} %fusion.83, bf16[2,3,512,1024]{3,2,1,0:T(8,128)(2,1)} %get-tuple-element.547, s32[]{:T(128)} %get-tuple-element.527, pred[]{:T(512)S(6)} %compare.3, bf16[1024,3,128]{0,2,1:T(8,128)(2,1)} %get-tuple-element.546, ...), kind=kOutput, calls=%fused_computation.26.clone.1 | convolution fusion | flops 414452224 | bytes 22414340 | tf_op jit(solution)/shard_map/while/body/eval_jaxpr/hqk,qhd->khd/dot_general | solution.py:95
  256.2 9.3 %fusion.84 = f32[2,512,3,128]{3,1,2,0:T(8,128)} fusion(f32[2,512,3,128]{3,1,2,0:T(8,128)} %get-tuple-element.530, s32[]{:T(128)} %get-tuple-element.527, bf16[1024,3,128]{2,0,1:T(8,128)(2,1)} %get-tuple-element.550, f32[3,512,1024]{2,1,0:T(8,128)} %fusion.83, bf16[2,3,512,1024]{3,2,1,0:T(8,128)(2,1)} %get-tuple-element.547), kind=kOutput, calls=%fused_computation.28.clone.1 | convolution fusion | flops 413665792 | bytes 20448768 | tf_op jit(solution)/shard_map/while/body/eval_jaxpr/hqk,khd->qhd/dot_general | solution.py:98
  265.5 2.9 bitcast_add_fusion.5
  268.5 3.7 copy.156
  272.2 2.7 copy.159
  274.9 3.0 copy.160
  277.9 2.3 multiply_reduce_fusion.3
  281.9 3.3 reshape.179
  285.3 4.3 fusion.47
  289.5 6.7 %all-to-all-start.3 = ((bf16[8,128,384]{1,2,0:T(8,128)(2,1)}), bf16[8,128,384]{1,2,0:T(8,128)(2,1)}, u32[]{:S(2)}, u32[]{:S(2)}) async-start(bf16[8,128,384]{1,2,0:T(8,128)(2,1)} %fusion.47), calls=%async_computation.3 | async-start | bytes 1572864 | tf_op jit(solution)/shard_map/all_to_all | solution.py:110
  296.2 2.0 multiply_reduce_fusion
  300.3 17.9 %all-to-all-done.3 = bf16[8,128,384]{1,2,0:T(8,128)(2,1)} async-done(((bf16[8,128,384]{1,2,0:T(8,128)(2,1)}), bf16[8,128,384]{1,2,0:T(8,128)(2,1)}, u32[]{:S(2)}, u32[]{:S(2)}) %all-to-all-start.3) | async-done | bytes 786464 | tf_op jit(solution)/shard_map/all_to_all | solution.py:110
  318.2 4.9 %all-to-all-start.4 = ((bf16[8,128,384]{2,1,0:T(8,128)(2,1)}), bf16[8,128,384]{2,1,0:T(8,128)(2,1)S(1)}, u32[]{:S(2)}, u32[]{:S(2)}) async-start(bf16[8,128,384]{2,1,0:T(8,128)(2,1)} %copy.163), calls=%async_computation.4 | async-start | bytes 1572864 | tf_op jit(solution)/shard_map/all_to_all | solution.py:113
  324.8 18.6 %all-to-all-done.4 = bf16[8,128,384]{2,1,0:T(8,128)(2,1)S(1)} async-done(((bf16[8,128,384]{2,1,0:T(8,128)(2,1)}), bf16[8,128,384]{2,1,0:T(8,128)(2,1)S(1)}, u32[]{:S(2)}, u32[]{:S(2)}) %all-to-all-start.4) | async-done | bytes 786464 | tf_op jit(solution)/shard_map/all_to_all | solution.py:113
  343.4 5.5 %all-to-all-start.5 = ((bf16[8,128,384]{2,1,0:T(8,128)(2,1)}), bf16[8,128,384]{2,1,0:T(8,128)(2,1)}, u32[]{:S(2)}, u32[]{:S(2)}) async-start(bf16[8,128,384]{2,1,0:T(8,128)(2,1)} %copy.165), calls=%async_computation.5 | async-start | bytes 1572864 | tf_op jit(solution)/shard_map/all_to_all | solution.py:116
  349.0 1.9 reshape.184
  350.9 2.6 multiply_reduce_fusion.1
  353.6 2.4 copy.170
  357.5 11.9 %all-to-all-done.5 = bf16[8,128,384]{2,1,0:T(8,128)(2,1)} async-done(((bf16[8,128,384]{2,1,0:T(8,128)(2,1)}), bf16[8,128,384]{2,1,0:T(8,128)(2,1)}, u32[]{:S(2)}, u32[]{:S(2)}) %all-to-all-start.5) | async-done | bytes 786464 | tf_op jit(solution)/shard_map/all_to_all | solution.py:116
  373.6 13.2 %all-reduce.2 = (f32[]{:T(128)}, f32[128]{0:T(128)S(1)}, f32[128]{0:T(128)S(1)}) all-reduce(f32[]{:T(128)} %fusion.51, f32[128]{0:T(128)S(1)} %multiply_reduce_fusion.1, f32[128]{0:T(128)S(1)} %get-tuple-element.303), channel_id=1, replica_groups=mesh['dp_0'=4,'dp_1'=4,'dp_2'=2,'seq'=8] {'dp_0'}, use_global_device_ids=true, to_apply=%region_14.15 | all-reduce | flops 257 | bytes 2056 | tf_op jit(solution)/shard_map/psum | solution.py:16
  386.9 11.0 %all-reduce.1 = (f32[]{:T(128)}, f32[128]{0:T(128)S(1)}, f32[128]{0:T(128)S(1)}) all-reduce(f32[]{:T(128)} %get-tuple-element.347, f32[128]{0:T(128)S(1)} %get-tuple-element.348, f32[128]{0:T(128)S(1)} %get-tuple-element.349), channel_id=1, replica_groups=mesh['dp_0'=4,'dp_1'=4,'dp_2'=2,'seq'=8] {'dp_1'}, use_global_device_ids=true, to_apply=%region_15.16 | all-reduce | flops 257 | bytes 2056 | tf_op jit(solution)/shard_map/psum | solution.py:16
  397.9 3.1 all-reduce.3
  401.0 16.2 %all-reduce = (f32[]{:T(128)}, f32[128]{0:T(128)S(1)}, f32[128]{0:T(128)S(1)}) all-reduce(f32[]{:T(128)} %get-tuple-element.350, f32[128]{0:T(128)S(1)} %get-tuple-element.351, f32[128]{0:T(128)S(1)} %get-tuple-element.352), channel_id=1, replica_groups=mesh['dp_0'=4,'dp_1'=4,'dp_2'=2,'seq'=8] {'seq'}, use_global_device_ids=true, to_apply=%region_17.18 | all-reduce | flops 257 | bytes 2056 | tf_op jit(solution)/shard_map/psum | solution.py:16
  (113 shorter events, 45.3 us)
Async XLA Ops:
  7.2 1.1 copy-start.12
  7.2 181.7 %all-gather.3.cloned.1.call-start = ((), (), s32[]{:S(2)}) async-start(), calls=%async_computation.8 | async-start | bytes 14155776 | tf_op jit(solution)/shard_map/all_gather | solution.py:75
  8.3 9.7 %copy-start.13 = (bf16[1,128,3072]{2,1,0:T(8,128)(2,1)S(1)}, bf16[1,128,3072]{2,1,0:T(8,128)(2,1)}, u32[]{:S(2)}) copy-start(bf16[1,128,3072]{2,1,0:T(8,128)(2,1)} %param.13) | copy-start | bytes 2359300
  9.5 35.9 %all-to-all-start = ((bf16[128,8,384]{0,2,1:T(8,128)(2,1)}), bf16[128,8,384]{0,2,1:T(8,128)(2,1)S(1)}, u32[]{:S(2)}, u32[]{:S(2)}) async-start(bf16[128,8,384]{0,2,1:T(8,128)(2,1)} %bitcast.4), calls=%async_computation | async-start | bytes 1572864 | tf_op jit(solution)/shard_map/all_to_all | solution.py:44
  18.0 33.2 %copy-start.14 = (bf16[1,128,3072]{2,1,0:T(8,128)(2,1)S(1)}, bf16[1,128,3072]{2,1,0:T(8,128)(2,1)}, u32[]{:S(2)}) copy-start(bf16[1,128,3072]{2,1,0:T(8,128)(2,1)} %param.14) | copy-start | bytes 2359300
  45.4 42.6 %copy-start.7 = (bf16[128,8,384]{0,2,1:T(8,128)(2,1)}, bf16[128,8,384]{0,2,1:T(8,128)(2,1)S(1)}, u32[]{:S(2)}) copy-start(bf16[128,8,384]{0,2,1:T(8,128)(2,1)S(1)} %all-to-all-done) | copy-start | bytes 2359300
  45.4 37.0 %all-to-all-start.1 = ((bf16[128,8,384]{0,2,1:T(8,128)(2,1)}), bf16[128,8,384]{0,2,1:T(8,128)(2,1)S(1)}, u32[]{:S(2)}, u32[]{:S(2)}) async-start(bf16[128,8,384]{0,2,1:T(8,128)(2,1)} %bitcast.8), calls=%async_computation.1 | async-start | bytes 1572864 | tf_op jit(solution)/shard_map/all_to_all | solution.py:45
  51.2 36.5 %copy-start.18 = (f32[128]{0:T(128)S(1)}, f32[128]{0:T(128)}, u32[]{:S(2)}) copy-start(f32[128]{0:T(128)} %param.18) | copy-start | bytes 1540
  51.2 36.5 %copy-start.19 = (s32[1,4]{1,0:T(1,128)S(1)}, s32[1,4]{1,0:T(1,128)}, u32[]{:S(2)}) copy-start(s32[1,4]{1,0:T(1,128)} %param.16) | copy-start | bytes 52
  82.4 5.6 %copy-start.11 = (bf16[128,8,384]{0,2,1:T(8,128)(2,1)}, bf16[128,8,384]{0,2,1:T(8,128)(2,1)S(1)}, u32[]{:S(2)}) copy-start(bf16[128,8,384]{0,2,1:T(8,128)(2,1)S(1)} %all-to-all-done.1) | copy-start | bytes 2359300
  82.4 36.3 %all-to-all-start.2 = ((bf16[128,8,384]{0,2,1:T(8,128)(2,1)}), bf16[128,8,384]{0,2,1:T(8,128)(2,1)}, u32[]{:S(2)}, u32[]{:S(2)}) async-start(bf16[128,8,384]{0,2,1:T(8,128)(2,1)} %bitcast.10), calls=%async_computation.2 | async-start | bytes 1572864 | tf_op jit(solution)/shard_map/all_to_all | solution.py:46
  87.7 284.4 %reduce-scatter.2.cloned.1.call-start = ((), (), s32[]{:S(2)}) async-start(), calls=%async_computation.7 | async-start | bytes 4866048 | tf_op jit(solution)/shard_map/reduce_scatter | solution.py:120
  89.0 1.7 copy-start.4
  95.6 0.7 copy-start.17
  125.7 1.9 copy-start.3
  130.5 3.5 copy-start
  134.0 1.9 copy-start.2
  134.0 1.9 copy-start.15
  135.9 2.6 copy-start.1
  138.5 0.9 copy-start.16
  141.1 3.5 copy-start
  144.5 1.9 copy-start.2
  144.5 1.9 copy-start.15
  146.5 2.6 copy-start.1
  149.1 0.9 copy-start.16
  289.5 28.7 %all-to-all-start.3 = ((bf16[8,128,384]{1,2,0:T(8,128)(2,1)}), bf16[8,128,384]{1,2,0:T(8,128)(2,1)}, u32[]{:S(2)}, u32[]{:S(2)}) async-start(bf16[8,128,384]{1,2,0:T(8,128)(2,1)} %fusion.47), calls=%async_computation.3 | async-start | bytes 1572864 | tf_op jit(solution)/shard_map/all_to_all | solution.py:110
  296.2 2.0 copy-start.8
  318.2 25.2 %all-to-all-start.4 = ((bf16[8,128,384]{2,1,0:T(8,128)(2,1)}), bf16[8,128,384]{2,1,0:T(8,128)(2,1)S(1)}, u32[]{:S(2)}, u32[]{:S(2)}) async-start(bf16[8,128,384]{2,1,0:T(8,128)(2,1)} %copy.163), calls=%async_computation.4 | async-start | bytes 1572864 | tf_op jit(solution)/shard_map/all_to_all | solution.py:113
  323.4 25.6 %copy-start.5 = (f32[8,128,384]{1,0,2:T(8,128)S(1)}, f32[8,128,384]{1,0,2:T(8,128)}, u32[]{:S(2)}) copy-start(f32[8,128,384]{1,0,2:T(8,128)} %copy-done.4) | copy-start | bytes 4718596
  343.4 5.5 %copy-start.9 = (bf16[8,128,384]{2,1,0:T(8,128)(2,1)}, bf16[8,128,384]{2,1,0:T(8,128)(2,1)S(1)}, u32[]{:S(2)}) copy-start(bf16[8,128,384]{2,1,0:T(8,128)(2,1)S(1)} %all-to-all-done.4) | copy-start | bytes 2359300
  343.4 25.9 %all-to-all-start.5 = ((bf16[8,128,384]{2,1,0:T(8,128)(2,1)}), bf16[8,128,384]{2,1,0:T(8,128)(2,1)}, u32[]{:S(2)}, u32[]{:S(2)}) async-start(bf16[8,128,384]{2,1,0:T(8,128)(2,1)} %copy.165), calls=%async_computation.5 | async-start | bytes 1572864 | tf_op jit(solution)/shard_map/all_to_all | solution.py:116
  349.0 1.9 copy-start.6
  353.6 2.4 copy-start.10
Sparse Core Ops, SparseCore 0:
  9.8 179.0 all-gather.2
  200.5 91.9 reduce-scatter.1
where the time goes:
time: 432 us; the launch traced here: 430 us
  waiting for transfers between devices  156 us (36%)
  matrix products  86.1 us (20%)
  local copies, waits for them, and re-layouts  60.2 us (14%)
  blocking collectives  43.5 us (10%)
  starting transfers between devices  36.9 us (9%)
  other arithmetic  26.9 us (6%)
  between operations  17.5 us (4%)
    psum x4, blocking collectives, one_axis_at_a_time(): array = lax.psum(array, axis)  43.5 us
    all_gather x1, waiting for transfers between devices, local(): out_full = lax.all_gather(out_grad[0], 'seq', axis=0, tiled=True)  32.1 us
    all_to_all x1, waiting for transfers between devices, local(): lax.all_to_all(key_rows[0], 'seq', split_axis=1, concat_axis=0, tiled=True)  30 us
    all_to_all x1, waiting for transfers between devices, local(): lax.all_to_all(query_rows[0], 'seq', split_axis=1, concat_axis=0, tiled=T...  26.2 us
    dot_general x2, matrix products, backward_block(): jnp.einsum('hqk,qhd->khd', d_scores, query_block, preferred_element_type=...  20.3 us
    all_to_all x1, waiting for transfers between devices, local(): lax.all_to_all(value_rows[0], 'seq', split_axis=1, concat_axis=0, tiled=T...  19.1 us
    dot_general x2, matrix products, backward_block(): jnp.einsum('hqk,khd->qhd', d_scores, k_norm, preferred_element_type=jnp.f...  19 us
    all_to_all x1, waiting for transfers between devices, local(): lax.all_to_all(key_grad.reshape(total, width), 'seq', split_axis=0, conca...  18.6 us
  transfers between devices with their start and end apart: 8, of which 7 were waited for; matrix products, arithmetic and copies ran while one was open for 35% of the time, Pallas kernels for 0%

commit v1 on v0

--- a/solution.py
+++ b/solution.py
@@ -40,9 +40,18 @@
 def local(
     query_rows, key_rows, value_rows, out_grad, clip_lengths, out_weight, query_gain, key_gain
 ):
+    things_read = lambda row_data: jnp.concatenate(
+        jax.lax.all_to_all(
+            jnp.stack(jnp.split(row_data, jax.lax.axis_size("seq"), axis=1)),
+            axis_name="seq",
+            split_axis=0,
+            concat_axis=0,
+        ),
+        axis=0,
+    )
     query, keys, values = (
         lax.all_to_all(query_rows[0], "seq", split_axis=1, concat_axis=0, tiled=True),
-        lax.all_to_all(key_rows[0], "seq", split_axis=1, concat_axis=0, tiled=True),
+        things_read(key_rows[0]),
         lax.all_to_all(value_rows[0], "seq", split_axis=1, concat_axis=0, tiled=True),
     )
     total = query.shape[0]

time: 432 us -> 419 us (0.970)
  waiting for transfers between devices: 156 us -> 143 us
  local copies, waits for them, and re-layouts: 60.2 us -> 65.7 us
    all_to_all x1, waiting for transfers between devices: 18.6 us -> 3.09 us  [local(): lax.all_to_all(key_grad.reshape(total, width), 'seq', split_axis=0, conca...]
    unnamed x41 -> x43, local copies, waits for them, and re-layouts: 14.8 us -> 19.4 us
  transfers between devices with their start and end apart: 8 -> 8, of which waited for: 7 -> 7; matrix products, arithmetic and copies ran while one was open for 35% -> 37% of each run, Pallas kernels for 0% -> 0%
where the time goes in v1:
time: 419 us; the launch traced here: 418 us
  waiting for transfers between devices  143 us (34%)
  matrix products  85.8 us (20%)
  local copies, waits for them, and re-layouts  65.7 us (16%)
  blocking collectives  41.7 us (10%)
  starting transfers between devices  35.4 us (8%)
  other arithmetic  26.3 us (6%)
  between operations  17.5 us (4%)
    psum x4, blocking collectives, one_axis_at_a_time(): array = lax.psum(array, axis)  41.7 us
    all_gather x1, waiting for transfers between devices, local(): out_full = lax.all_gather(out_grad[0], 'seq', axis=0, tiled=True)  32 us
    all_to_all x1, waiting for transfers between devices, local(): lax.all_to_all(query_rows[0], 'seq', split_axis=1, concat_axis=0, tiled=T...  30 us
    all_to_all x1, waiting for transfers between devices, local(): jax.lax.all_to_all(jnp.stack(jnp.split(row_data, jax.lax.axis_size('seq')...  28.7 us
    dot_general x2, matrix products, backward_block(): jnp.einsum('hqk,qhd->khd', d_scores, query_block, preferred_element_type=...  20.1 us
    unnamed x43, local copies, waits for them, and re-layouts  19.4 us
    dot_general x2, matrix products, backward_block(): jnp.einsum('hqk,khd->qhd', d_scores, k_norm, preferred_element_type=jnp.f...  19 us
    all_to_all x1, waiting for transfers between devices, local(): lax.all_to_all(query_grad.reshape(total, width), 'seq', split_axis=0, con...  18.1 us
  transfers between devices with their start and end apart: 8, of which 7 were waited for; matrix products, arithmetic and copies ran while one was open for 37% of the time, Pallas kernels for 0%

profile of v1, /device:TPU:32, one launch (start us, length us, event | category | flops | bytes accessed | tf_op | source)
XLA Modules:
  0.0 418.0 jit_solution(7598361986365479915)
XLA Ops:
  13.5 8.6 %all-to-all-start.1 = ((bf16[8,128,384]{2,1,0:T(8,128)(2,1)}), bf16[8,128,384]{2,1,0:T(8,128)(2,1)S(1)}, u32[]{:S(2)}, u32[]{:S(2)}) async-start(bf16[8,128,384]{2,1,0:T(8,128)(2,1)} %fusion.52), calls=%async_computation.1 | async-start | bytes 1572864 | tf_op jit(solution)/shard_map/all_to_all | solution.py:44
  23.2 28.7 %all-to-all-done.1 = bf16[8,128,384]{2,1,0:T(8,128)(2,1)S(1)} async-done(((bf16[8,128,384]{2,1,0:T(8,128)(2,1)}), bf16[8,128,384]{2,1,0:T(8,128)(2,1)S(1)}, u32[]{:S(2)}, u32[]{:S(2)}) %all-to-all-start.1) | async-done | bytes 786464 | tf_op jit(solution)/shard_map/all_to_all | solution.py:44
  51.9 5.1 %all-to-all-start = ((bf16[128,8,384]{0,2,1:T(8,128)(2,1)}), bf16[128,8,384]{0,2,1:T(8,128)(2,1)S(1)}, u32[]{:S(2)}, u32[]{:S(2)}) async-start(bf16[128,8,384]{0,2,1:T(8,128)(2,1)} %bitcast.4), calls=%async_computation | async-start | bytes 1572864 | tf_op jit(solution)/shard_map/all_to_all | solution.py:53
  58.2 30.0 %all-to-all-done = bf16[128,8,384]{0,2,1:T(8,128)(2,1)S(1)} async-done(((bf16[128,8,384]{0,2,1:T(8,128)(2,1)}), bf16[128,8,384]{0,2,1:T(8,128)(2,1)S(1)}, u32[]{:S(2)}, u32[]{:S(2)}) %all-to-all-start) | async-done | bytes 786464 | tf_op jit(solution)/shard_map/all_to_all | solution.py:53
  88.2 5.3 %all-to-all-start.2 = ((bf16[128,8,384]{0,2,1:T(8,128)(2,1)}), bf16[128,8,384]{0,2,1:T(8,128)(2,1)}, u32[]{:S(2)}, u32[]{:S(2)}) async-start(bf16[128,8,384]{0,2,1:T(8,128)(2,1)} %bitcast.17), calls=%async_computation.2 | async-start | bytes 1572864 | tf_op jit(solution)/shard_map/all_to_all | solution.py:55
  98.7 2.3 copy.149
  102.3 2.1 copy.144
  104.3 2.6 reshape.176
  106.9 17.6 %all-to-all-done.2 = bf16[128,8,384]{0,2,1:T(8,128)(2,1)} async-done(((bf16[128,8,384]{0,2,1:T(8,128)(2,1)}), bf16[128,8,384]{0,2,1:T(8,128)(2,1)}, u32[]{:S(2)}, u32[]{:S(2)}) %all-to-all-start.2) | async-done | bytes 786464 | tf_op jit(solution)/shard_map/all_to_all | solution.py:55
  124.5 2.5 copy.147
  127.0 2.2 reshape.171
  129.2 2.3 copy.150
  134.6 21.1 %while.27 = (s32[]{:T(128)}, bf16[2,3,512,1024]{3,2,1,0:T(8,128)(2,1)}, bf16[2,512,3,128]{3,1,2,0:T(8,128)(2,1)}, s32[2]{0:T(128)S(1)}, s32[1024]{0:T(1024)S(1)}...) while((s32[]{:T(128)}, ...), condition=%wide.region_6.7_spmd, body=%wide.region_4.6_spmd.sunk | while | flops 817035776 | bytes 85746000 | solution.py:82
  136.3 3.4 fusion.83
  146.8 3.5 fusion.83
  155.7 3.1 copy.165
  158.8 2.2 copy.178
  160.9 32.0 %all-gather.3.cloned.1.call-done = bf16[1,1024,6144]{2,1,0:T(8,128)(2,1)} async-done(((bf16[1,128,6144]{2,1,0:T(8,128)(2,1)}), bf16[1,1024,6144]{2,1,0:T(8,128)(2,1)}) %all-gather.3.cloned.1.call-update) | async-done | bytes 12582928 | tf_op jit(solution)/shard_map/all_gather | solution.py:84
  192.9 11.4 %fusion.42 = bf16[384,6144]{0,1:T(8,128)(2,1)} fusion(bf16[1024,384]{0,1:T(8,128)(2,1)} %bitcast.199, bf16[1,1024,6144]{2,1,0:T(8,128)(2,1)} %all-gather.3.cloned.1.call-done), kind=kOutput, calls=%fused_computation.45 | convolution fusion | flops 4834197504 | bytes 18087936 | tf_op jit(solution)/shard_map/dot_general | solution.py:85
  204.3 10.4 %fusion.48 = bf16[1024,384]{0,1:T(8,128)(2,1)} fusion(bf16[384,6144]{1,0:T(8,128)(2,1)} %param.17, bf16[1,1024,6144]{2,1,0:T(8,128)(2,1)} %all-gather.3.cloned.1.call-done), kind=kOutput, calls=%fused_computation.61 | convolution fusion | flops 4832231424 | bytes 18087936 | tf_op jit(solution)/shard_map/dot_general | solution.py:86
  214.7 57.5 %while.28 = (s32[]{:T(128)}, f32[1024,3,128]{0,2,1:T(8,128)}, f32[1024,3,128]{0,2,1:T(8,128)S(1)}, f32[2,512,3,128]{3,1,2,0:T(8,128)}, s32[2]{0:T(128)S(1)}, /*i...) while((s32[]{:T(128)}, f32[1024,3,128]{0,2,1:T(8,128)}, ...), condition=%wide.region_9.10_spmd.clone, body=%wide.region_7.9_spmd.clone.sunk | while | flops 1634210816 | bytes 57019604 | solution.py:111
  216.0 5.0 %fusion.91 = f32[3,512,1024]{2,1,0:T(8,128)} fusion(bf16[1024,3,128]{2,0,1:T(8,128)(2,1)} %get-tuple-element.549, bf16[1024,3,128]{0,2,1:T(8,128)(2,1)} %get-tuple-element.548, s32[]{:T(128)S(6)} %select_n.24), kind=kOutput, calls=%fused_computation.30.clone.1 | convolution fusion | flops 402653184 | bytes 7471108 | tf_op jit(solution)/shard_map/while/body/eval_jaxpr/qhd,khd->hqk/dot_general | solution.py:97
  220.9 10.1 %bitcast_add_fusion.4 = f32[1024,3,128]{0,2,1:T(8,128)} fusion(f32[1024,3,128]{0,2,1:T(8,128)} %get-tuple-element.528, f32[3,512,1024]{2,1,0:T(8,128)} %fusion.91, bf16[2,3,512,1024]{3,2,1,0:T(8,128)(2,1)} %get-tuple-element.547, s32[]{:T(128)} %get-tuple-element.527, pred[]{:T(512)S(6)} %compare.3, bf16[1024,3,128]{0,2,1:T(8,128)(2,1)} %get-tuple-element.546, ...), kind=kOutput, calls=%fused_computation.26.clone.1 | convolution fusion | flops 414452224 | bytes 22414340 | tf_op jit(solution)/shard_map/while/body/eval_jaxpr/hqk,qhd->khd/dot_general | solution.py:104
  231.1 9.7 %fusion.92 = f32[2,512,3,128]{3,1,2,0:T(8,128)} fusion(f32[2,512,3,128]{3,1,2,0:T(8,128)} %get-tuple-element.530, s32[]{:T(128)} %get-tuple-element.527, bf16[1024,3,128]{2,0,1:T(8,128)(2,1)} %get-tuple-element.550, f32[3,512,1024]{2,1,0:T(8,128)} %fusion.91, bf16[2,3,512,1024]{3,2,1,0:T(8,128)(2,1)} %get-tuple-element.547), kind=kOutput, calls=%fused_computation.28.clone.1 | convolution fusion | flops 413665792 | bytes 20448768 | tf_op jit(solution)/shard_map/while/body/eval_jaxpr/hqk,khd->qhd/dot_general | solution.py:107
  240.7 3.0 bitcast_add_fusion.5
  245.0 4.9 %fusion.91 = f32[3,512,1024]{2,1,0:T(8,128)} fusion(bf16[1024,3,128]{2,0,1:T(8,128)(2,1)} %get-tuple-element.549, bf16[1024,3,128]{0,2,1:T(8,128)(2,1)} %get-tuple-element.548, s32[]{:T(128)S(6)} %select_n.24), kind=kOutput, calls=%fused_computation.30.clone.1 | convolution fusion | flops 402653184 | bytes 7471108 | tf_op jit(solution)/shard_map/while/body/eval_jaxpr/qhd,khd->hqk/dot_general | solution.py:97
  250.0 10.0 %bitcast_add_fusion.4 = f32[1024,3,128]{0,2,1:T(8,128)} fusion(f32[1024,3,128]{0,2,1:T(8,128)} %get-tuple-element.528, f32[3,512,1024]{2,1,0:T(8,128)} %fusion.91, bf16[2,3,512,1024]{3,2,1,0:T(8,128)(2,1)} %get-tuple-element.547, s32[]{:T(128)} %get-tuple-element.527, pred[]{:T(512)S(6)} %compare.3, bf16[1024,3,128]{0,2,1:T(8,128)(2,1)} %get-tuple-element.546, ...), kind=kOutput, calls=%fused_computation.26.clone.1 | convolution fusion | flops 414452224 | bytes 22414340 | tf_op jit(solution)/shard_map/while/body/eval_jaxpr/hqk,qhd->khd/dot_general | solution.py:104
  260.0 9.3 %fusion.92 = f32[2,512,3,128]{3,1,2,0:T(8,128)} fusion(f32[2,512,3,128]{3,1,2,0:T(8,128)} %get-tuple-element.530, s32[]{:T(128)} %get-tuple-element.527, bf16[1024,3,128]{2,0,1:T(8,128)(2,1)} %get-tuple-element.550, f32[3,512,1024]{2,1,0:T(8,128)} %fusion.91, bf16[2,3,512,1024]{3,2,1,0:T(8,128)(2,1)} %get-tuple-element.547), kind=kOutput, calls=%fused_computation.28.clone.1 | convolution fusion | flops 413665792 | bytes 20448768 | tf_op jit(solution)/shard_map/while/body/eval_jaxpr/hqk,khd->qhd/dot_general | solution.py:107
  269.3 2.9 bitcast_add_fusion.5
  272.3 2.0 multiply_reduce_fusion
  276.3 6.7 %all-to-all-start.4 = ((bf16[8,128,384]{2,1,0:T(8,128)(2,1)}), bf16[8,128,384]{2,1,0:T(8,128)(2,1)}, u32[]{:S(2)}, u32[]{:S(2)}) async-start(bf16[8,128,384]{2,1,0:T(8,128)(2,1)} %copy.161), calls=%async_computation.4 | async-start | bytes 1572864 | tf_op jit(solution)/shard_map/all_to_all | solution.py:122
  285.0 2.1 copy.154
  288.4 3.2 copy.158
  295.3 2.4 reshape.173
  297.7 4.3 %fusion.47 = bf16[8,128,384]{1,2,0:T(8,128)(2,1)} fusion(f32[8,128,384]{1,0,2:T(8,128)} %bitcast.183, f32[8,128,384]{1,0,2:T(8,128)} %reshape.173, f32[8,128,384]{1,0,2:T(8,128)} %bitcast.182, f32[384]{0:T(512)S(1)} %broadcast_bitcast_fusion, bf16[128,8,384]{0,2,1:T(8,128)(2,1)} %copy-done.7), kind=kLoop, calls=%fused_computation.49 | loop fusion | flops 2752512 | bytes 6292992 | tf_op jit(solution)/shard_map/convert_element_type | solution.py:37
  301.9 3.1 all-to-all-done.4
  305.0 4.2 all-to-all-start.3
  310.4 2.5 copy.163
  312.9 18.1 %all-to-all-done.3 = bf16[8,128,384]{1,2,0:T(8,128)(2,1)} async-done(((bf16[8,128,384]{1,2,0:T(8,128)(2,1)}), bf16[8,128,384]{1,2,0:T(8,128)(2,1)}, u32[]{:S(2)}, u32[]{:S(2)}) %all-to-all-start.3) | async-done | bytes 786464 | tf_op jit(solution)/shard_map/all_to_all | solution.py:119
  331.0 5.5 %all-to-all-start.5 = ((bf16[8,128,384]{2,1,0:T(8,128)(2,1)}), bf16[8,128,384]{2,1,0:T(8,128)(2,1)}, u32[]{:S(2)}, u32[]{:S(2)}) async-start(bf16[8,128,384]{2,1,0:T(8,128)(2,1)} %copy.163), calls=%async_computation.5 | async-start | bytes 1572864 | tf_op jit(solution)/shard_map/all_to_all | solution.py:125
  336.6 1.9 reshape.178
  338.5 2.6 multiply_reduce_fusion.1
  343.8 2.3 copy.168
  346.1 12.7 %all-to-all-done.5 = bf16[8,128,384]{2,1,0:T(8,128)(2,1)} async-done(((bf16[8,128,384]{2,1,0:T(8,128)(2,1)}), bf16[8,128,384]{2,1,0:T(8,128)(2,1)}, u32[]{:S(2)}, u32[]{:S(2)}) %all-to-all-start.5) | async-done | bytes 786464 | tf_op jit(solution)/shard_map/all_to_all | solution.py:125
  363.0 9.9 %all-reduce.2 = (f32[]{:T(128)}, f32[128]{0:T(128)S(1)}, f32[128]{0:T(128)S(1)}) all-reduce(f32[]{:T(128)} %fusion.51, f32[128]{0:T(128)S(1)} %multiply_reduce_fusion.1, f32[128]{0:T(128)S(1)} %get-tuple-element.303), channel_id=1, replica_groups=mesh['dp_0'=4,'dp_1'=4,'dp_2'=2,'seq'=8] {'dp_0'}, use_global_device_ids=true, to_apply=%region_14.15 | all-reduce | flops 257 | bytes 2056 | tf_op jit(solution)/shard_map/psum | solution.py:16
  372.9 12.5 %all-reduce.1 = (f32[]{:T(128)}, f32[128]{0:T(128)S(1)}, f32[128]{0:T(128)S(1)}) all-reduce(f32[]{:T(128)} %get-tuple-element.347, f32[128]{0:T(128)S(1)} %get-tuple-element.348, f32[128]{0:T(128)S(1)} %get-tuple-element.349), channel_id=1, replica_groups=mesh['dp_0'=4,'dp_1'=4,'dp_2'=2,'seq'=8] {'dp_1'}, use_global_device_ids=true, to_apply=%region_15.16 | all-reduce | flops 257 | bytes 2056 | tf_op jit(solution)/shard_map/psum | solution.py:16
  385.4 3.1 all-reduce.3
  388.5 16.2 %all-reduce = (f32[]{:T(128)}, f32[128]{0:T(128)S(1)}, f32[128]{0:T(128)S(1)}) all-reduce(f32[]{:T(128)} %get-tuple-element.350, f32[128]{0:T(128)S(1)} %get-tuple-element.351, f32[128]{0:T(128)S(1)} %get-tuple-element.352), channel_id=1, replica_groups=mesh['dp_0'=4,'dp_1'=4,'dp_2'=2,'seq'=8] {'seq'}, use_global_device_ids=true, to_apply=%region_17.18 | all-reduce | flops 257 | bytes 2056 | tf_op jit(solution)/shard_map/psum | solution.py:16
  (115 shorter events, 52.3 us)
Async XLA Ops:
  7.2 1.1 copy-start.10
  7.2 185.8 %all-gather.3.cloned.1.call-start = ((), (), s32[]{:S(2)}) async-start(), calls=%async_computation.8 | async-start | bytes 14155776 | tf_op jit(solution)/shard_map/all_gather | solution.py:84
  8.3 13.8 %copy-start.11 = (bf16[1,128,3072]{2,1,0:T(8,128)(2,1)S(1)}, bf16[1,128,3072]{2,1,0:T(8,128)(2,1)}, u32[]{:S(2)}) copy-start(bf16[1,128,3072]{2,1,0:T(8,128)(2,1)} %param.12) | copy-start | bytes 2359300
  13.5 38.4 %all-to-all-start.1 = ((bf16[8,128,384]{2,1,0:T(8,128)(2,1)}), bf16[8,128,384]{2,1,0:T(8,128)(2,1)S(1)}, u32[]{:S(2)}, u32[]{:S(2)}) async-start(bf16[8,128,384]{2,1,0:T(8,128)(2,1)} %fusion.52), calls=%async_computation.1 | async-start | bytes 1572864 | tf_op jit(solution)/shard_map/all_to_all | solution.py:44
  22.1 34.9 %copy-start.12 = (bf16[1,128,3072]{2,1,0:T(8,128)(2,1)S(1)}, bf16[1,128,3072]{2,1,0:T(8,128)(2,1)}, u32[]{:S(2)}) copy-start(bf16[1,128,3072]{2,1,0:T(8,128)(2,1)} %param.14) | copy-start | bytes 2359300
  51.9 36.3 %all-to-all-start = ((bf16[128,8,384]{0,2,1:T(8,128)(2,1)}), bf16[128,8,384]{0,2,1:T(8,128)(2,1)S(1)}, u32[]{:S(2)}, u32[]{:S(2)}) async-start(bf16[128,8,384]{0,2,1:T(8,128)(2,1)} %bitcast.4), calls=%async_computation | async-start | bytes 1572864 | tf_op jit(solution)/shard_map/all_to_all | solution.py:53
  57.0 36.5 %copy-start.17 = (s32[1,4]{1,0:T(1,128)S(1)}, s32[1,4]{1,0:T(1,128)}, u32[]{:S(2)}) copy-start(s32[1,4]{1,0:T(1,128)} %param.16) | copy-start | bytes 52
  88.2 5.3 %copy-start.7 = (bf16[128,8,384]{0,2,1:T(8,128)(2,1)}, bf16[128,8,384]{0,2,1:T(8,128)(2,1)S(1)}, u32[]{:S(2)}) copy-start(bf16[128,8,384]{0,2,1:T(8,128)(2,1)S(1)} %all-to-all-done) | copy-start | bytes 2359300
  88.2 36.3 %all-to-all-start.2 = ((bf16[128,8,384]{0,2,1:T(8,128)(2,1)}), bf16[128,8,384]{0,2,1:T(8,128)(2,1)}, u32[]{:S(2)}, u32[]{:S(2)}) async-start(bf16[128,8,384]{0,2,1:T(8,128)(2,1)} %bitcast.17), calls=%async_computation.2 | async-start | bytes 1572864 | tf_op jit(solution)/shard_map/all_to_all | solution.py:55
  93.5 268.0 %reduce-scatter.2.cloned.1.call-start = ((), (), s32[]{:S(2)}) async-start(), calls=%async_computation.7 | async-start | bytes 4866048 | tf_op jit(solution)/shard_map/reduce_scatter | solution.py:129
  96.9 0.7 copy-start.15
  129.2 4.0 copy-start.16
  131.6 1.9 copy-start.3
  136.3 3.4 copy-start
  139.7 1.9 copy-start.2
  139.7 1.9 copy-start.13
  141.7 2.6 copy-start.1
  144.3 0.9 copy-start.14
  146.8 3.5 copy-start
  150.3 1.9 copy-start.2
  150.3 1.9 copy-start.13
  152.2 2.6 copy-start.1
  154.8 0.9 copy-start.14
  272.2 2.1 copy-start.8
  276.3 28.7 %all-to-all-start.4 = ((bf16[8,128,384]{2,1,0:T(8,128)(2,1)}), bf16[8,128,384]{2,1,0:T(8,128)(2,1)}, u32[]{:S(2)}, u32[]{:S(2)}) async-start(bf16[8,128,384]{2,1,0:T(8,128)(2,1)} %copy.161), calls=%async_computation.4 | async-start | bytes 1572864 | tf_op jit(solution)/shard_map/all_to_all | solution.py:122
  283.3 1.8 copy-start.9
  288.4 3.2 copy-start.4
  293.5 1.7 copy-start.6
  305.0 26.0 %all-to-all-start.3 = ((bf16[8,128,384]{1,2,0:T(8,128)(2,1)}), bf16[8,128,384]{1,2,0:T(8,128)(2,1)}, u32[]{:S(2)}, u32[]{:S(2)}) async-start(bf16[8,128,384]{1,2,0:T(8,128)(2,1)} %fusion.47), calls=%async_computation.3 | async-start | bytes 1572864 | tf_op jit(solution)/shard_map/all_to_all | solution.py:119
  310.4 26.2 %copy-start.5 = (f32[8,128,384]{1,0,2:T(8,128)S(1)}, f32[8,128,384]{1,0,2:T(8,128)}, u32[]{:S(2)}) copy-start(f32[8,128,384]{1,0,2:T(8,128)} %copy.144) | copy-start | bytes 4718596
  331.0 27.8 %all-to-all-start.5 = ((bf16[8,128,384]{2,1,0:T(8,128)(2,1)}), bf16[8,128,384]{2,1,0:T(8,128)(2,1)}, u32[]{:S(2)}, u32[]{:S(2)}) async-start(bf16[8,128,384]{2,1,0:T(8,128)(2,1)} %copy.163), calls=%async_computation.5 | async-start | bytes 1572864 | tf_op jit(solution)/shard_map/all_to_all | solution.py:125
Sparse Core Ops, SparseCore 0:
  9.8 183.1 all-gather.2
  204.5 91.9 reduce-scatter.1
